TPU v7x, 32 devices: a whole 2x2x4 slice. The times are simulated.
32 devices in a mesh: gx: 4 (over z), gy: 4 (over y, core), gz: 2 (over x).
Axes of the slice: x: 2, y: 2, z: 4, core: 2. Of those that a mesh axis runs over, the one named last changes fastest.
Arguments:
- right_side: float32 [128, 128, 256], P('gx', 'gy', 'gz'), may hold values from -8 to 8
- guess: float32 [128, 128, 256], P('gx', 'gy', 'gz'), may hold values from -4 to 4
Outputs:
- solution_field: float32 [128, 128, 256], P('gx', 'gy', 'gz')
- residual: float32 [128, 128, 256], P('gx', 'gy', 'gz')
All inputs are finite; a program needn't handle non-finite values.
Results may differ from a plain program's by a relative error of at most 0.0001.
Values sent between devices are 32-bit elements; how exact they have to be, the bound alone decides.
A program may use at most 128 MiB of HBM per device.

v0:
```python
import jax
import jax.numpy as jnp
from jax import lax
from jax.sharding import PartitionSpec as P

LEVELS = 6
SWEEPS = 4
STEPS = 2
damping = 2.0 / 3.0


def passed_along(value, axis, steps):
    count = lax.axis_size(axis)
    first, last = (max(0, -steps), min(count, count - steps))
    return lax.ppermute(value, axis, [(source, source + steps) for source in range(first, last)])


def padded_2(x, sides, width):
    for axis, dim in sides:
        count, length = (lax.axis_size(axis), x.shape[dim])
        up = [(i, (i + 1) % count) for i in range(count - 1)]
        down = [(j, i) for i, j in up]
        last = lax.slice_in_dim(x, length - width, length, axis=dim)
        first = lax.slice_in_dim(x, 0, width, axis=dim)
        before = lax.ppermute(last, axis, up)
        after = lax.ppermute(first, axis, down)
        x = jnp.concatenate([before, x, after], axis=dim)
    return x


def padded_stencil(padded):
    beside = padded[2:, 1:-1, 1:-1] + padded[:-2, 1:-1, 1:-1]
    beside = beside + padded[1:-1, 2:, 1:-1] + padded[1:-1, :-2, 1:-1]
    beside = beside + padded[1:-1, 1:-1, 2:] + padded[1:-1, 1:-1, :-2]
    return 6.0 * padded[1:-1, 1:-1, 1:-1] - beside


def restrict(field):
    first, second, third = field.shape
    blocks = field.reshape(first // 2, 2, second // 2, 2, third // 2, 2)
    return jnp.mean(blocks, axis=(1, 3, 5))


def prolong(field):
    first, second, third = field.shape
    spread = jnp.broadcast_to(field[:, None, :, None, :, None], (first, 2, second, 2, third, 2))
    return spread.reshape(first * 2, second * 2, third * 2)


def axis_layers(packed, axis_name, by):
    if axis_name == "gx":
        return passed_along(packed, "gx", by)
    if axis_name == "gy":
        return passed_along(packed, "gy", by)
    return passed_along(packed, "gz", by)


def extend_all(fields, margin):
    current = list(fields)
    for dim_index, axis_name in ((0, "gx"), (1, "gy"), (2, "gz")):
        lows = [lax.slice_in_dim(f, 0, margin, axis=dim_index) for f in current]
        highs = [
            lax.slice_in_dim(f, f.shape[dim_index] - margin, f.shape[dim_index], axis=dim_index)
            for f in current
        ]
        received = {}
        for by in (1, -1):
            pieces = highs if by == 1 else lows
            packed = jnp.concatenate([p.reshape(-1) for p in pieces])
            received[by] = axis_layers(packed, axis_name, by)
        grown = []
        offset = 0
        for index, field in enumerate(current):
            piece_shape = lows[index].shape
            count = lows[index].size
            from_lower = received[1][offset : offset + count].reshape(piece_shape)
            from_upper = received[-1][offset : offset + count].reshape(piece_shape)
            offset = offset + count
            grown.append(jnp.concatenate([from_lower, field, from_upper], axis=dim_index))
        current = grown
    return current


def smooth_merged(items):
    results = {}
    approxes = [damping * rhs / (6.0 * 0.25**lev) for rhs, lev in items]
    for sweep_index in range(SWEEPS - 1):
        padded_list = extend_all(approxes, 1)
        renewed = []
        for index, (rhs, lev) in enumerate(items):
            scaling = 0.25**lev
            diagonal_value = 6.0 * scaling
            renewed.append(
                approxes[index]
                + damping * (rhs - scaling * padded_stencil(padded_list[index])) / diagonal_value
            )
        approxes = renewed
    for index, (rhs, lev) in enumerate(items):
        results[lev] = approxes[index]
    return results


def precondition(residual):
    chain = [residual]
    for level_index in range(1, LEVELS):
        chain.append(restrict(chain[-1]))
    first_level = LEVELS - 1
    local_levels = list(range(first_level + 1))
    smoothed = smooth_merged([(chain[lev], lev) for lev in local_levels])
    correction = smoothed[first_level]
    for level_index in range(first_level - 1, -1, -1):
        correction = prolong(correction) + smoothed[level_index]
    return correction


def apply_fine(field):
    padded = padded_2(field, (("gx", 0), ("gy", 1), ("gz", 2)), 1)
    return padded_stencil(padded)


def shards(right_side, guess):
    solution_field = guess
    residual = right_side - apply_fine(guess)
    for step_index in range(STEPS):
        direction = precondition(residual)
        image = apply_fine(direction)
        along, curvature = lax.psum(
            (jnp.sum(residual * direction), jnp.sum(direction * image)), ("gx", "gy", "gz")
        )
        alpha = along / curvature
        solution_field = solution_field + alpha * direction
        residual = residual - alpha * image
    return (solution_field, residual)


def solution(mesh):
    placed = (P("gx", "gy", "gz"), P("gx", "gy", "gz"))
    return jax.shard_map(
        shards,
        mesh=mesh,
        in_specs=placed,
        out_specs=(P("gx", "gy", "gz"), P("gx", "gy", "gz")),
        check_vma=False,
    )
```

profile of v0, /device:TPU:0, one launch (start us, length us, event | category | flops | bytes accessed | tf_op | source)
XLA Modules:
  0.0 606.6 jit_solution(4249604036732145625)
XLA Ops:
  2.7 5.6 collective-permute-start.1
  11.0 3.0 collective-permute-start.3
  17.2 4.5 collective-permute-start.5
  23.5 1.8 broadcast_multiply_fusion.1
  25.7 34.9 %reshape.1638 = f32[16,2,16,2,64,2]{5,4,3,2,1,0:T(8,128)} reshape(f32[32,32,128]{2,1,0:T(8,128)S(1)} %copy.405) | data formatting | bytes 1048576 | tf_op jit(solution)/shard_map/reshape | solution.py:40
  60.5 12.2 %reduce_sum.140 = f32[16,16,64]{2,1,0:T(8,128)S(1)} reduce(f32[16,2,16,2,64,2]{5,4,3,2,1,0:T(8,128)} %reshape.1638, f32[]{:T(128)} %constant.169.clone.1), dimensions={1,3,5}, to_apply=%region_0.0 | reduce | flops 114688 | bytes 589828 | tf_op jit(solution)/shard_map/reduce_sum | solution.py:41
  72.8 5.6 div.223
  78.4 2.6 reduce_sum.141
  82.3 4.2 collective-permute-start.7
  88.3 4.3 collective-permute-done.6
  97.4 5.7 collective-permute-done.8
  109.0 4.7 collective-permute-start.11
  122.3 3.5 collective-permute-start.13
  128.3 4.4 collective-permute-done.12
  134.3 2.0 collective-permute-start.15
  138.2 3.5 collective-permute-done.14
  147.7 4.5 collective-permute-start.17
  163.2 3.5 collective-permute-start.19
  170.4 4.4 collective-permute-done.18
  176.4 2.0 collective-permute-start.21
  180.3 3.5 collective-permute-done.20
  190.2 4.9 collective-permute-start.23
  201.7 2.5 broadcast_in_dim.38
  204.2 4.9 reshape.1846
  210.7 11.4 %broadcast_in_dim.39 = f32[16,2,16,2,64,2]{5,4,3,2,1,0:T(8,128)} broadcast(f32[16,16,64]{2,1,0:T(8,128)S(1)} %fusion.112), dimensions={0,2,4} | broadcast | bytes 589824 | tf_op jit(solution)/shard_map/broadcast_in_dim | solution.py:46
  222.0 24.1 %reshape.1849 = f32[32,32,128]{2,1,0:T(8,128)S(1)} reshape(f32[16,2,16,2,64,2]{5,4,3,2,1,0:T(8,128)} %broadcast_in_dim.39) | data formatting | bytes 1048576 | tf_op jit(solution)/shard_map/reshape | solution.py:47
  247.1 1.5 fusion.45
  250.0 4.5 collective-permute-start.25
  257.3 3.0 collective-permute-start.27
  263.5 4.5 collective-permute-start.29
  271.1 45.0 %all-reduce.1 = (f32[]{:T(128)}, f32[]{:T(128)}) all-reduce(f32[]{:T(128)} %get-tuple-element.9, f32[]{:T(128)} %get-tuple-element.8), channel_id=1, replica_groups=mesh['gx'=4,'gy'=4,'gz'=2] {'gx','gy','gz'}, use_global_device_ids=true, to_apply=%region_7.0 | all-reduce | flops 2 | bytes 16 | tf_op jit(solution)/shard_map/psum | solution.py:127
  317.9 34.9 %reshape.1852 = f32[16,2,16,2,64,2]{5,4,3,2,1,0:T(8,128)} reshape(f32[32,32,128]{2,1,0:T(8,128)S(1)} %copy.511) | data formatting | bytes 1048576 | tf_op jit(solution)/shard_map/reshape | solution.py:40
  352.7 12.2 %reduce_sum.149 = f32[16,16,64]{2,1,0:T(8,128)S(1)} reduce(f32[16,2,16,2,64,2]{5,4,3,2,1,0:T(8,128)} %reshape.1852, f32[]{:T(128)} %constant.169.clone.1), dimensions={1,3,5}, to_apply=%region_10.0 | reduce | flops 114688 | bytes 589828 | tf_op jit(solution)/shard_map/reduce_sum | solution.py:41
  365.0 5.6 div.269
  370.6 2.6 reduce_sum.150
  374.5 1.8 collective-permute-start.31
  378.1 4.3 collective-permute-done.30
  387.2 4.3 collective-permute-done.32
  395.3 1.5 copy.517
  399.4 4.5 collective-permute-start.35
  410.0 1.7 fusion.29
  412.0 2.6 collective-permute-start.37
  416.4 4.3 collective-permute-done.36
  422.3 2.2 collective-permute-start.39
  424.9 1.5 collective-permute-start.38
  426.5 3.2 collective-permute-done.38
  437.6 4.5 collective-permute-start.41
  448.3 1.7 fusion.20
  450.2 3.9 collective-permute-start.43
  455.9 4.4 collective-permute-done.42
  461.9 2.0 collective-permute-start.45
  465.8 3.5 collective-permute-done.44
  477.2 4.8 collective-permute-start.47
  485.6 2.5 broadcast_in_dim.86
  488.1 4.9 reshape.2060
  493.8 11.4 %broadcast_in_dim.87 = f32[16,2,16,2,64,2]{5,4,3,2,1,0:T(8,128)} broadcast(f32[16,16,64]{2,1,0:T(8,128)S(1)} %fusion.81), dimensions={0,2,4} | broadcast | bytes 589824 | tf_op jit(solution)/shard_map/broadcast_in_dim | solution.py:46
  505.1 24.5 %reshape.2063 = f32[32,32,128]{2,1,0:T(8,128)} reshape(f32[16,2,16,2,64,2]{5,4,3,2,1,0:T(8,128)} %broadcast_in_dim.87) | data formatting | bytes 1048576 | tf_op jit(solution)/shard_map/reshape | solution.py:47
  530.6 1.9 fusion.11
  533.8 4.5 collective-permute-start.49
  541.1 3.0 collective-permute-start.51
  547.9 4.5 collective-permute-start.53
  554.3 2.1 multiply_reduce_fusion
  556.4 44.8 %all-reduce = (f32[]{:T(128)}, f32[]{:T(128)}) all-reduce(f32[]{:T(128)} %get-tuple-element.7, f32[]{:T(128)} %get-tuple-element.6), channel_id=1, replica_groups=mesh['gx'=4,'gy'=4,'gz'=2] {'gx','gy','gz'}, use_global_device_ids=true, to_apply=%region_17.0 | all-reduce | flops 2 | bytes 16 | tf_op jit(solution)/shard_map/psum | solution.py:127
  602.5 1.5 multiply_subtract_fusion
  (1008 shorter events, 155.5 us)
Async XLA Ops:
  1.4 8.2 %collective-permute-start = (f32[1,32,128]{2,0,1:T(1,128)S(1)}, f32[1,32,128]{2,0,1:T(1,128)S(1)}, u32[]{:S(2)}, u32[]{:S(2)}) collective-permute-start(f32[1,32,128]{2,0,1:T(1,128)S(1)} %bitcast.399), channel_id=1, source_target_pairs={{8,0},{16,8},{24,16},{9,1},{17,9},{25,17},{10,2},{18,10},{26,18},{... | collective-permute-start | bytes 49160 | tf_op jit(solution)/shard_map/ppermute | solution.py:26
  2.7 7.0 %collective-permute-start.1 = (f32[1,32,128]{2,0,1:T(1,128)S(1)}, f32[1,32,128]{2,0,1:T(1,128)S(1)}, u32[]{:S(2)}, u32[]{:S(2)}) collective-permute-start(f32[1,32,128]{2,0,1:T(1,128)S(1)} %bitcast.398), channel_id=1, source_target_pairs={{0,8},{8,16},{16,24},{1,9},{9,17},{17,25},{2,10},{10,18},{18,26},{... | collective-permute-start | bytes 49160 | tf_op jit(solution)/shard_map/ppermute | solution.py:25
  9.7 4.3 collective-permute-start.2
  11.0 3.9 collective-permute-start.3
  15.5 6.2 %collective-permute-start.4 = (f32[34,34,1]{1,2,0:T(1,128)S(1)}, f32[34,34,1]{1,2,0:T(1,128)S(1)}, u32[]{:S(2)}, u32[]{:S(2)}) collective-permute-start(f32[34,34,1]{1,2,0:T(1,128)S(1)} %copy.400), channel_id=1, source_target_pairs={{1,0},{3,2},{5,4},{7,6},{9,8},{11,10},{13,12},{15,14},{17,16},{19,... | collective-permute-start | bytes 13880 | tf_op jit(solution)/shard_map/ppermute | solution.py:26
  17.2 6.0 collective-permute-start.5
  81.6 74.1 %copy-start.7 = (f32[2,2,8]{2,1,0:T(2,128)}, f32[2,2,8]{2,1,0:T(2,128)S(1)}, u32[]{:S(2)}) copy-start(f32[2,2,8]{2,1,0:T(2,128)S(1)} %reduce_sum.143) | copy-start | bytes 388
  81.8 71.8 %copy-start.20 = (f32[4]{0:T(128)}, f32[4]{0:T(128)S(1)}, u32[]{:S(2)}) copy-start(f32[4]{0:T(128)S(1)} %reduce_sum.146) | copy-start | bytes 52
  82.3 5.9 collective-permute-start.7
  86.9 5.7 collective-permute-start.6
  88.3 14.9 %copy-start.21 = (f32[1,1,4]{2,1,0:T(1,128)}, f32[1,1,4]{2,1,0:T(1,128)S(1)}, u32[]{:S(2)}) copy-start(f32[1,1,4]{2,1,0:T(1,128)S(1)} %slice_bitcast_fusion.22) | copy-start | bytes 52
  94.2 3.0 collective-permute-start.9
  95.9 7.1 %collective-permute-start.8 = (f32[5964]{0:T(1024)S(1)}, f32[5964]{0:T(1024)S(1)}, u32[]{:S(2)}, u32[]{:S(2)}) collective-permute-start(f32[5964]{0:T(1024)S(1)} %concatenate.1027), channel_id=1, source_target_pairs={{2,0},{4,2},{6,4},{3,1},{5,3},{7,5},{10,8},{12,10},{14,12},{11,9},... | collective-permute-start | bytes 71576 | tf_op jit(solution)/shard_map/ppermute | solution.py:15
  106.6 7.2 %collective-permute-start.10 = (f32[1641]{0:T(1024)S(1)}, f32[1641]{0:T(1024)S(1)}, u32[]{:S(2)}, u32[]{:S(2)}) collective-permute-start(f32[1641]{0:T(1024)S(1)} %concatenate.1035), channel_id=1, source_target_pairs={{1,0},{3,2},{5,4},{7,6},{9,8},{11,10},{13,12},{15,14},{17,16},{19,... | collective-permute-start | bytes 19700 | tf_op jit(solution)/shard_map/ppermute | solution.py:15
  109.0 5.9 collective-permute-start.11
  121.6 22.0 %copy-start.17 = (f32[1,1,4]{2,1,0:T(1,128)}, f32[1,1,4]{2,1,0:T(1,128)S(1)}, u32[]{:S(2)}) copy-start(f32[1,1,4]{2,1,0:T(1,128)S(1)} %fusion.366) | copy-start | bytes 52
  122.3 5.9 collective-permute-start.13
  126.9 5.8 collective-permute-start.12
  134.3 3.7 collective-permute-start.15
  136.7 5.0 collective-permute-start.14
  138.0 22.4 %copy-start.10 = (f32[5964]{0:T(1024)}, f32[5964]{0:T(1024)S(1)}, u32[]{:S(2)}) copy-start(f32[5964]{0:T(1024)S(1)} %collective-permute-done.15) | copy-start | bytes 71572
  145.3 7.0 %collective-permute-start.16 = (f32[1641]{0:T(1024)S(1)}, f32[1641]{0:T(1024)S(1)}, u32[]{:S(2)}, u32[]{:S(2)}) collective-permute-start(f32[1641]{0:T(1024)S(1)} %concatenate.1085), channel_id=1, source_target_pairs={{1,0},{3,2},{5,4},{7,6},{9,8},{11,10},{13,12},{15,14},{17,16},{19,... | collective-permute-start | bytes 19700 | tf_op jit(solution)/shard_map/ppermute | solution.py:15
  147.7 5.9 collective-permute-start.17
  154.2 22.1 %copy-start.12 = (f32[2,2,8]{2,1,0:T(2,128)}, f32[2,2,8]{2,1,0:T(2,128)S(1)}, u32[]{:S(2)}) copy-start(f32[2,2,8]{2,1,0:T(2,128)S(1)} %multiply_add_fusion.3) | copy-start | bytes 388
  155.9 30.8 %copy-start.2 = (f32[4,4,16]{2,1,0:T(4,128)}, f32[4,4,16]{2,1,0:T(4,128)S(1)}, u32[]{:S(2)}) copy-start(f32[4,4,16]{2,1,0:T(4,128)S(1)} %fusion.258) | copy-start | bytes 3076
  163.2 7.2 %collective-permute-start.19 = (f32[5460]{0:T(1024)S(1)}, f32[5460]{0:T(1024)S(1)}, u32[]{:S(2)}, u32[]{:S(2)}) collective-permute-start(f32[5460]{0:T(1024)S(1)} %concatenate.1120), channel_id=1, source_target_pairs={{0,8},{8,16},{16,24},{1,9},{9,17},{17,25},{2,10},{10,18},{18,26},{... | collective-permute-start | bytes 65528 | tf_op jit(solution)/shard_map/ppermute | solution.py:15
  169.1 5.8 collective-permute-start.18
  176.4 3.7 collective-permute-start.21
  178.8 5.0 collective-permute-start.20
  186.3 14.3 %copy-start.3 = (f32[18,1,64]{2,1,0:T(1,128)}, f32[18,1,64]{2,1,0:T(1,128)S(1)}, u32[]{:S(2)}) copy-start(f32[18,1,64]{2,1,0:T(1,128)S(1)} %reshape.1817) | copy-start | bytes 13828
  186.4 14.2 %copy-start.4 = (f32[18,1,64]{2,1,0:T(1,128)}, f32[18,1,64]{2,1,0:T(1,128)S(1)}, u32[]{:S(2)}) copy-start(f32[18,1,64]{2,1,0:T(1,128)S(1)} %reshape.1818) | copy-start | bytes 13828
  187.7 7.4 %collective-permute-start.22 = (f32[1641]{0:T(1024)S(1)}, f32[1641]{0:T(1024)S(1)}, u32[]{:S(2)}, u32[]{:S(2)}) collective-permute-start(f32[1641]{0:T(1024)S(1)} %concatenate.1135), channel_id=1, source_target_pairs={{1,0},{3,2},{5,4},{7,6},{9,8},{11,10},{13,12},{15,14},{17,16},{19,... | collective-permute-start | bytes 19700 | tf_op jit(solution)/shard_map/ppermute | solution.py:15
  190.2 5.9 collective-permute-start.23
  248.7 5.9 collective-permute-start.24
  250.0 6.0 collective-permute-start.25
  256.0 4.3 collective-permute-start.26
  257.3 3.9 collective-permute-start.27
  261.8 6.2 %collective-permute-start.28 = (f32[34,34,1]{1,2,0:T(1,128)S(1)}, f32[34,34,1]{1,2,0:T(1,128)S(1)}, u32[]{:S(2)}, u32[]{:S(2)}) collective-permute-start(f32[34,34,1]{1,2,0:T(1,128)S(1)} %copy.506), channel_id=1, source_target_pairs={{1,0},{3,2},{5,4},{7,6},{9,8},{11,10},{13,12},{15,14},{17,16},{19,... | collective-permute-start | bytes 13880 | tf_op jit(solution)/shard_map/ppermute | solution.py:26
  263.5 6.0 collective-permute-start.29
  374.5 3.5 collective-permute-start.31
  376.8 5.7 collective-permute-start.30
  384.0 3.0 collective-permute-start.33
  385.7 5.8 collective-permute-start.32
  397.0 7.0 %collective-permute-start.34 = (f32[1641]{0:T(1024)S(1)}, f32[1641]{0:T(1024)S(1)}, u32[]{:S(2)}, u32[]{:S(2)}) collective-permute-start(f32[1641]{0:T(1024)S(1)} %concatenate.1193), channel_id=1, source_target_pairs={{1,0},{3,2},{5,4},{7,6},{9,8},{11,10},{13,12},{15,14},{17,16},{19,... | collective-permute-start | bytes 19700 | tf_op jit(solution)/shard_map/ppermute | solution.py:15
  399.4 5.9 collective-permute-start.35
  412.0 4.3 collective-permute-start.37
  415.0 5.7 collective-permute-start.36
  422.3 4.1 collective-permute-start.39
  424.9 4.9 collective-permute-start.38
  435.2 7.0 %collective-permute-start.40 = (f32[1641]{0:T(1024)S(1)}, f32[1641]{0:T(1024)S(1)}, u32[]{:S(2)}, u32[]{:S(2)}) collective-permute-start(f32[1641]{0:T(1024)S(1)} %concatenate.1243), channel_id=1, source_target_pairs={{1,0},{3,2},{5,4},{7,6},{9,8},{11,10},{13,12},{15,14},{17,16},{19,... | collective-permute-start | bytes 19700 | tf_op jit(solution)/shard_map/ppermute | solution.py:15
  437.6 5.9 collective-permute-start.41
  450.2 5.6 collective-permute-start.43
  454.5 5.8 collective-permute-start.42
  461.9 3.7 collective-permute-start.45
  464.3 5.0 collective-permute-start.44
  471.9 57.6 %copy-start.1 = (f32[34,1,128]{2,0,1:T(8,128)}, f32[34,1,128]{2,0,1:T(8,128)S(1)}, u32[]{:S(2)}) copy-start(f32[34,1,128]{2,0,1:T(8,128)S(1)} %slice_bitcast_fusion) | copy-start | bytes 52228
  474.8 7.2 %collective-permute-start.46 = (f32[1641]{0:T(1024)S(1)}, f32[1641]{0:T(1024)S(1)}, u32[]{:S(2)}, u32[]{:S(2)}) collective-permute-start(f32[1641]{0:T(1024)S(1)} %concatenate.1293), channel_id=1, source_target_pairs={{1,0},{3,2},{5,4},{7,6},{9,8},{11,10},{13,12},{15,14},{17,16},{19,... | collective-permute-start | bytes 19700 | tf_op jit(solution)/shard_map/ppermute | solution.py:15
  477.2 5.9 collective-permute-start.47
  532.5 5.9 collective-permute-start.48
  533.8 6.0 collective-permute-start.49
  539.8 4.3 collective-permute-start.50
  541.1 3.9 collective-permute-start.51
  546.2 6.2 %collective-permute-start.52 = (f32[34,34,1]{1,2,0:T(1,128)S(1)}, f32[34,34,1]{1,2,0:T(1,128)S(1)}, u32[]{:S(2)}, u32[]{:S(2)}) collective-permute-start(f32[34,34,1]{1,2,0:T(1,128)S(1)} %copy.612), channel_id=1, source_target_pairs={{1,0},{3,2},{5,4},{7,6},{9,8},{11,10},{13,12},{15,14},{17,16},{19,... | collective-permute-start | bytes 13880 | tf_op jit(solution)/shard_map/ppermute | solution.py:26
  547.9 6.0 collective-permute-start.53
  (15 other events, 103.3 us)
where the time goes:
time: 617 us; the launch traced here: 607 us
  local copies, waits for them, and re-layouts  258 us (42%)
  starting transfers between devices  131 us (21%)
  blocking collectives  89.7 us (15%)
  waiting for transfers between devices  64.4 us (10%)
  other arithmetic  57.4 us (9%)
  between operations  6.56 us (1%)
    psum x2, blocking collectives, shards(): lax.psum((jnp.sum(residual * direction), jnp.sum(direction * image)), ('g...  89.7 us
    ppermute x36, starting transfers between devices, passed_along(): lax.ppermute(value, axis, [(source, source + steps) for source in range(f...  81.6 us
    reshape x2, local copies, waits for them, and re-layouts, restrict(): blocks = field.reshape(first // 2, 2, second // 2, 2, third // 2, 2)  69.7 us
    reshape x8, local copies, waits for them, and re-layouts, prolong(): return spread.reshape(first * 2, second * 2, third * 2)  58.9 us
    ppermute x36, waiting for transfers between devices, passed_along(): lax.ppermute(value, axis, [(source, source + steps) for source in range(f...  56 us
    ppermute x9, starting transfers between devices, padded_2(): before = lax.ppermute(last, axis, up)  37.4 us
    reduce_sum x12, other arithmetic, restrict(): return jnp.mean(blocks, axis=(1, 3, 5))  30.3 us
    broadcast_in_dim x12, local copies, waits for them, and re-layouts, prolong(): jnp.broadcast_to(field[:, None, :, None, :, None], (first, 2, second, 2,...  28.4 us
  transfers between devices with their start and end apart: 54, of which 27 were waited for; matrix products, arithmetic and copies ran while one was open for 3% of the time, Pallas kernels for 0%

commit v1 on v0

--- a/solution.py
+++ b/solution.py
@@ -125,7 +125,8 @@
         direction = precondition(residual)
         image = apply_fine(direction)
         along, curvature = lax.psum(
-            (jnp.sum(residual * direction), jnp.sum(direction * image)), ("gx", "gy", "gz")
+            lax.psum((jnp.sum(residual * direction), jnp.sum(direction * image)), "gx"),
+            ("gy", "gz"),
         )
         alpha = along / curvature
         solution_field = solution_field + alpha * direction

time: 617 us -> 582 us (0.943)
  blocking collectives: 89.7 us -> 56.8 us
    psum x2 -> x4, blocking collectives: 89.7 us -> 56.8 us  [the longest x2 34.1 us: shards(): lax.psum(lax.psum((jnp.sum(residual * direction), jnp.sum(direction * ima...]
where the time goes in v1:
time: 582 us; the launch traced here: 572 us
  local copies, waits for them, and re-layouts  258 us (44%)
  starting transfers between devices  128 us (22%)
  waiting for transfers between devices  64.6 us (11%)
  other arithmetic  57.4 us (10%)
  blocking collectives  56.8 us (10%)
  between operations  6.5 us (1%)
    ppermute x36, starting transfers between devices, passed_along(): lax.ppermute(value, axis, [(source, source + steps) for source in range(f...  79.4 us
    reshape x2, local copies, waits for them, and re-layouts, restrict(): blocks = field.reshape(first // 2, 2, second // 2, 2, third // 2, 2)  69.7 us
    reshape x8, local copies, waits for them, and re-layouts, prolong(): return spread.reshape(first * 2, second * 2, third * 2)  58.9 us
    ppermute x36, waiting for transfers between devices, passed_along(): lax.ppermute(value, axis, [(source, source + steps) for source in range(f...  56.2 us
    ppermute x9, starting transfers between devices, padded_2(): before = lax.ppermute(last, axis, up)  37.4 us
    psum x2, blocking collectives, shards(): lax.psum(lax.psum((jnp.sum(residual * direction), jnp.sum(direction * ima...  34.1 us
    reduce_sum x12, other arithmetic, restrict(): return jnp.mean(blocks, axis=(1, 3, 5))  30.3 us
    broadcast_in_dim x12, local copies, waits for them, and re-layouts, prolong(): jnp.broadcast_to(field[:, None, :, None, :, None], (first, 2, second, 2,...  28.4 us
  transfers between devices with their start and end apart: 54, of which 27 were waited for; matrix products, arithmetic and copies ran while one was open for 3% of the time, Pallas kernels for 0%

profile of v1, /device:TPU:0, one launch (start us, length us, event | category | flops | bytes accessed | tf_op | source)
XLA Modules:
  0.0 571.6 jit_solution(3017431412340355313)
XLA Ops:
  2.7 5.6 collective-permute-start.1
  11.0 3.0 collective-permute-start.3
  17.2 4.5 collective-permute-start.5
  23.5 1.8 broadcast_multiply_fusion.1
  25.7 34.9 %reshape.1638 = f32[16,2,16,2,64,2]{5,4,3,2,1,0:T(8,128)} reshape(f32[32,32,128]{2,1,0:T(8,128)S(1)} %copy.405) | data formatting | bytes 1048576 | tf_op jit(solution)/shard_map/reshape | solution.py:40
  60.5 12.2 %reduce_sum.140 = f32[16,16,64]{2,1,0:T(8,128)S(1)} reduce(f32[16,2,16,2,64,2]{5,4,3,2,1,0:T(8,128)} %reshape.1638, f32[]{:T(128)} %constant.169.clone.1), dimensions={1,3,5}, to_apply=%region_0.0 | reduce | flops 114688 | bytes 589828 | tf_op jit(solution)/shard_map/reduce_sum | solution.py:41
  72.8 5.6 div.223
  78.4 2.6 reduce_sum.141
  82.3 4.2 collective-permute-start.7
  88.3 4.3 collective-permute-done.6
  97.4 5.7 collective-permute-done.8
  109.0 4.7 collective-permute-start.11
  122.3 3.5 collective-permute-start.13
  128.3 4.4 collective-permute-done.12
  134.3 2.0 collective-permute-start.15
  138.2 3.5 collective-permute-done.14
  147.7 4.5 collective-permute-start.17
  163.2 3.5 collective-permute-start.19
  170.4 4.4 collective-permute-done.18
  176.4 2.0 collective-permute-start.21
  180.3 3.5 collective-permute-done.20
  190.2 4.9 collective-permute-start.23
  201.7 2.5 broadcast_in_dim.38
  204.2 4.9 reshape.1846
  210.7 11.4 %broadcast_in_dim.39 = f32[16,2,16,2,64,2]{5,4,3,2,1,0:T(8,128)} broadcast(f32[16,16,64]{2,1,0:T(8,128)S(1)} %fusion.112), dimensions={0,2,4} | broadcast | bytes 589824 | tf_op jit(solution)/shard_map/broadcast_in_dim | solution.py:46
  222.0 24.1 %reshape.1849 = f32[32,32,128]{2,1,0:T(8,128)S(1)} reshape(f32[16,2,16,2,64,2]{5,4,3,2,1,0:T(8,128)} %broadcast_in_dim.39) | data formatting | bytes 1048576 | tf_op jit(solution)/shard_map/reshape | solution.py:47
  247.1 1.5 fusion.45
  250.0 4.5 collective-permute-start.25
  257.3 3.0 collective-permute-start.27
  263.5 4.5 collective-permute-start.29
  271.1 11.3 %all-reduce.3 = (f32[]{:T(128)}, f32[]{:T(128)}) all-reduce(f32[]{:T(128)} %get-tuple-element.9, f32[]{:T(128)} %get-tuple-element.8), channel_id=1, replica_groups=mesh['gx'=4,'gy'=4,'gz'=2] {'gx'}, use_global_device_ids=true, to_apply=%region_7.0 | all-reduce | flops 2 | bytes 16 | tf_op jit(solution)/shard_map/psum | solution.py:128
  282.5 17.1 %all-reduce.1 = (f32[]{:T(128)}, f32[]{:T(128)}) all-reduce(f32[]{:T(128)} %get-tuple-element.100, f32[]{:T(128)} %get-tuple-element.101), channel_id=1, replica_groups=mesh['gx'=4,'gy'=4,'gz'=2] {'gy','gz'}, use_global_device_ids=true, to_apply=%region_8.0 | all-reduce | flops 2 | bytes 16 | tf_op jit(solution)/shard_map/psum | solution.py:127
  301.4 34.9 %reshape.1852 = f32[16,2,16,2,64,2]{5,4,3,2,1,0:T(8,128)} reshape(f32[32,32,128]{2,1,0:T(8,128)S(1)} %copy.511) | data formatting | bytes 1048576 | tf_op jit(solution)/shard_map/reshape | solution.py:40
  336.3 12.2 %reduce_sum.149 = f32[16,16,64]{2,1,0:T(8,128)S(1)} reduce(f32[16,2,16,2,64,2]{5,4,3,2,1,0:T(8,128)} %reshape.1852, f32[]{:T(128)} %constant.169.clone.1), dimensions={1,3,5}, to_apply=%region_12.0 | reduce | flops 114688 | bytes 589828 | tf_op jit(solution)/shard_map/reduce_sum | solution.py:41
  348.5 5.6 div.269
  354.1 2.6 reduce_sum.150
  358.0 1.6 collective-permute-start.31
  361.4 4.3 collective-permute-done.30
  370.4 3.9 collective-permute-done.32
  382.3 4.5 collective-permute-start.35
  392.9 1.7 fusion.29
  394.9 2.4 collective-permute-start.37
  399.0 4.4 collective-permute-done.36
  405.0 2.0 collective-permute-start.39
  408.9 3.5 collective-permute-done.38
  417.9 1.5 collective-permute-start.40
  420.5 4.5 collective-permute-start.41
  431.2 1.7 fusion.20
  433.1 2.6 collective-permute-start.43
  437.5 4.4 collective-permute-done.42
  443.4 2.0 collective-permute-start.45
  447.3 3.5 collective-permute-done.44
  458.7 4.5 collective-permute-start.47
  467.1 2.5 broadcast_in_dim.86
  469.6 4.9 reshape.2060
  475.3 11.4 %broadcast_in_dim.87 = f32[16,2,16,2,64,2]{5,4,3,2,1,0:T(8,128)} broadcast(f32[16,16,64]{2,1,0:T(8,128)S(1)} %fusion.81), dimensions={0,2,4} | broadcast | bytes 589824 | tf_op jit(solution)/shard_map/broadcast_in_dim | solution.py:46
  486.7 24.5 %reshape.2063 = f32[32,32,128]{2,1,0:T(8,128)} reshape(f32[16,2,16,2,64,2]{5,4,3,2,1,0:T(8,128)} %broadcast_in_dim.87) | data formatting | bytes 1048576 | tf_op jit(solution)/shard_map/reshape | solution.py:47
  512.1 1.9 fusion.11
  515.3 4.5 collective-permute-start.49
  522.6 3.0 collective-permute-start.51
  529.4 4.5 collective-permute-start.53
  535.8 2.1 multiply_reduce_fusion
  537.9 11.3 %all-reduce.2 = (f32[]{:T(128)}, f32[]{:T(128)}) all-reduce(f32[]{:T(128)} %get-tuple-element.7, f32[]{:T(128)} %get-tuple-element.6), channel_id=1, replica_groups=mesh['gx'=4,'gy'=4,'gz'=2] {'gx'}, use_global_device_ids=true, to_apply=%region_19.0 | all-reduce | flops 2 | bytes 16 | tf_op jit(solution)/shard_map/psum | solution.py:128
  549.2 17.0 %all-reduce = (f32[]{:T(128)}, f32[]{:T(128)}) all-reduce(f32[]{:T(128)} %get-tuple-element.98, f32[]{:T(128)} %get-tuple-element.99), channel_id=1, replica_groups=mesh['gx'=4,'gy'=4,'gz'=2] {'gy','gz'}, use_global_device_ids=true, to_apply=%region_20.0 | all-reduce | flops 2 | bytes 16 | tf_op jit(solution)/shard_map/psum | solution.py:127
  (1010 shorter events, 158.8 us)
Async XLA Ops:
  1.4 8.2 %collective-permute-start = (f32[1,32,128]{2,0,1:T(1,128)S(1)}, f32[1,32,128]{2,0,1:T(1,128)S(1)}, u32[]{:S(2)}, u32[]{:S(2)}) collective-permute-start(f32[1,32,128]{2,0,1:T(1,128)S(1)} %bitcast.399), channel_id=1, source_target_pairs={{8,0},{16,8},{24,16},{9,1},{17,9},{25,17},{10,2},{18,10},{26,18},{... | collective-permute-start | bytes 49160 | tf_op jit(solution)/shard_map/ppermute | solution.py:26
  2.7 7.0 %collective-permute-start.1 = (f32[1,32,128]{2,0,1:T(1,128)S(1)}, f32[1,32,128]{2,0,1:T(1,128)S(1)}, u32[]{:S(2)}, u32[]{:S(2)}) collective-permute-start(f32[1,32,128]{2,0,1:T(1,128)S(1)} %bitcast.398), channel_id=1, source_target_pairs={{0,8},{8,16},{16,24},{1,9},{9,17},{17,25},{2,10},{10,18},{18,26},{... | collective-permute-start | bytes 49160 | tf_op jit(solution)/shard_map/ppermute | solution.py:25
  9.7 4.3 collective-permute-start.2
  11.0 3.9 collective-permute-start.3
  15.5 6.2 %collective-permute-start.4 = (f32[34,34,1]{1,2,0:T(1,128)S(1)}, f32[34,34,1]{1,2,0:T(1,128)S(1)}, u32[]{:S(2)}, u32[]{:S(2)}) collective-permute-start(f32[34,34,1]{1,2,0:T(1,128)S(1)} %copy.400), channel_id=1, source_target_pairs={{1,0},{3,2},{5,4},{7,6},{9,8},{11,10},{13,12},{15,14},{17,16},{19,... | collective-permute-start | bytes 13880 | tf_op jit(solution)/shard_map/ppermute | solution.py:26
  17.2 6.0 %collective-permute-start.5 = (f32[34,34,1]{1,2,0:T(1,128)S(1)}, f32[34,34,1]{1,2,0:T(1,128)S(1)}, u32[]{:S(2)}, u32[]{:S(2)}) collective-permute-start(f32[34,34,1]{1,2,0:T(1,128)S(1)} %copy.402), channel_id=1, source_target_pairs={{0,1},{2,3},{4,5},{6,7},{8,9},{10,11},{12,13},{14,15},{16,17},{18,... | collective-permute-start | bytes 13880 | tf_op jit(solution)/shard_map/ppermute | solution.py:25
  81.6 74.1 %copy-start.7 = (f32[2,2,8]{2,1,0:T(2,128)}, f32[2,2,8]{2,1,0:T(2,128)S(1)}, u32[]{:S(2)}) copy-start(f32[2,2,8]{2,1,0:T(2,128)S(1)} %reduce_sum.143) | copy-start | bytes 388
  81.8 71.8 %copy-start.20 = (f32[4]{0:T(128)}, f32[4]{0:T(128)S(1)}, u32[]{:S(2)}) copy-start(f32[4]{0:T(128)S(1)} %reduce_sum.146) | copy-start | bytes 52
  82.3 5.9 %collective-permute-start.7 = (f32[5460]{0:T(1024)S(1)}, f32[5460]{0:T(1024)S(1)}, u32[]{:S(2)}, u32[]{:S(2)}) collective-permute-start(f32[5460]{0:T(1024)S(1)} %concatenate.1020), channel_id=1, source_target_pairs={{0,8},{8,16},{16,24},{1,9},{9,17},{17,25},{2,10},{10,18},{18,26},{... | collective-permute-start | bytes 65528 | tf_op jit(solution)/shard_map/ppermute | solution.py:15
  86.9 5.7 collective-permute-start.6
  88.3 14.9 %copy-start.21 = (f32[1,1,4]{2,1,0:T(1,128)}, f32[1,1,4]{2,1,0:T(1,128)S(1)}, u32[]{:S(2)}) copy-start(f32[1,1,4]{2,1,0:T(1,128)S(1)} %slice_bitcast_fusion.22) | copy-start | bytes 52
  94.2 3.0 collective-permute-start.9
  95.9 7.1 %collective-permute-start.8 = (f32[5964]{0:T(1024)S(1)}, f32[5964]{0:T(1024)S(1)}, u32[]{:S(2)}, u32[]{:S(2)}) collective-permute-start(f32[5964]{0:T(1024)S(1)} %concatenate.1027), channel_id=1, source_target_pairs={{2,0},{4,2},{6,4},{3,1},{5,3},{7,5},{10,8},{12,10},{14,12},{11,9},... | collective-permute-start | bytes 71576 | tf_op jit(solution)/shard_map/ppermute | solution.py:15
  106.6 7.2 %collective-permute-start.10 = (f32[1641]{0:T(1024)S(1)}, f32[1641]{0:T(1024)S(1)}, u32[]{:S(2)}, u32[]{:S(2)}) collective-permute-start(f32[1641]{0:T(1024)S(1)} %concatenate.1035), channel_id=1, source_target_pairs={{1,0},{3,2},{5,4},{7,6},{9,8},{11,10},{13,12},{15,14},{17,16},{19,... | collective-permute-start | bytes 19700 | tf_op jit(solution)/shard_map/ppermute | solution.py:15
  109.0 5.9 %collective-permute-start.11 = (f32[1641]{0:T(1024)S(1)}, f32[1641]{0:T(1024)S(1)}, u32[]{:S(2)}, u32[]{:S(2)}) collective-permute-start(f32[1641]{0:T(1024)S(1)} %concatenate.1037), channel_id=1, source_target_pairs={{0,1},{2,3},{4,5},{6,7},{8,9},{10,11},{12,13},{14,15},{16,17},{18,... | collective-permute-start | bytes 19700 | tf_op jit(solution)/shard_map/ppermute | solution.py:15
  121.6 22.0 %copy-start.17 = (f32[1,1,4]{2,1,0:T(1,128)}, f32[1,1,4]{2,1,0:T(1,128)S(1)}, u32[]{:S(2)}) copy-start(f32[1,1,4]{2,1,0:T(1,128)S(1)} %fusion.366) | copy-start | bytes 52
  122.3 5.9 %collective-permute-start.13 = (f32[5460]{0:T(1024)S(1)}, f32[5460]{0:T(1024)S(1)}, u32[]{:S(2)}, u32[]{:S(2)}) collective-permute-start(f32[5460]{0:T(1024)S(1)} %concatenate.1070), channel_id=1, source_target_pairs={{0,8},{8,16},{16,24},{1,9},{9,17},{17,25},{2,10},{10,18},{18,26},{... | collective-permute-start | bytes 65528 | tf_op jit(solution)/shard_map/ppermute | solution.py:15
  126.9 5.8 %collective-permute-start.12 = (f32[5460]{0:T(1024)S(1)}, f32[5460]{0:T(1024)S(1)}, u32[]{:S(2)}, u32[]{:S(2)}) collective-permute-start(f32[5460]{0:T(1024)S(1)} %concatenate.1069), channel_id=1, source_target_pairs={{8,0},{16,8},{24,16},{9,1},{17,9},{25,17},{10,2},{18,10},{26,18},{... | collective-permute-start | bytes 65528 | tf_op jit(solution)/shard_map/ppermute | solution.py:15
  134.3 3.7 collective-permute-start.15
  136.7 5.0 collective-permute-start.14
  138.0 22.4 %copy-start.10 = (f32[5964]{0:T(1024)}, f32[5964]{0:T(1024)S(1)}, u32[]{:S(2)}) copy-start(f32[5964]{0:T(1024)S(1)} %collective-permute-done.15) | copy-start | bytes 71572
  145.3 7.0 %collective-permute-start.16 = (f32[1641]{0:T(1024)S(1)}, f32[1641]{0:T(1024)S(1)}, u32[]{:S(2)}, u32[]{:S(2)}) collective-permute-start(f32[1641]{0:T(1024)S(1)} %concatenate.1085), channel_id=1, source_target_pairs={{1,0},{3,2},{5,4},{7,6},{9,8},{11,10},{13,12},{15,14},{17,16},{19,... | collective-permute-start | bytes 19700 | tf_op jit(solution)/shard_map/ppermute | solution.py:15
  147.7 5.9 %collective-permute-start.17 = (f32[1641]{0:T(1024)S(1)}, f32[1641]{0:T(1024)S(1)}, u32[]{:S(2)}, u32[]{:S(2)}) collective-permute-start(f32[1641]{0:T(1024)S(1)} %concatenate.1087), channel_id=1, source_target_pairs={{0,1},{2,3},{4,5},{6,7},{8,9},{10,11},{12,13},{14,15},{16,17},{18,... | collective-permute-start | bytes 19700 | tf_op jit(solution)/shard_map/ppermute | solution.py:15
  154.2 22.1 %copy-start.12 = (f32[2,2,8]{2,1,0:T(2,128)}, f32[2,2,8]{2,1,0:T(2,128)S(1)}, u32[]{:S(2)}) copy-start(f32[2,2,8]{2,1,0:T(2,128)S(1)} %multiply_add_fusion.3) | copy-start | bytes 388
  155.9 30.8 %copy-start.2 = (f32[4,4,16]{2,1,0:T(4,128)}, f32[4,4,16]{2,1,0:T(4,128)S(1)}, u32[]{:S(2)}) copy-start(f32[4,4,16]{2,1,0:T(4,128)S(1)} %fusion.258) | copy-start | bytes 3076
  163.2 7.2 %collective-permute-start.19 = (f32[5460]{0:T(1024)S(1)}, f32[5460]{0:T(1024)S(1)}, u32[]{:S(2)}, u32[]{:S(2)}) collective-permute-start(f32[5460]{0:T(1024)S(1)} %concatenate.1120), channel_id=1, source_target_pairs={{0,8},{8,16},{16,24},{1,9},{9,17},{17,25},{2,10},{10,18},{18,26},{... | collective-permute-start | bytes 65528 | tf_op jit(solution)/shard_map/ppermute | solution.py:15
  169.1 5.8 %collective-permute-start.18 = (f32[5460]{0:T(1024)S(1)}, f32[5460]{0:T(1024)S(1)}, u32[]{:S(2)}, u32[]{:S(2)}) collective-permute-start(f32[5460]{0:T(1024)S(1)} %concatenate.1119), channel_id=1, source_target_pairs={{8,0},{16,8},{24,16},{9,1},{17,9},{25,17},{10,2},{18,10},{26,18},{... | collective-permute-start | bytes 65528 | tf_op jit(solution)/shard_map/ppermute | solution.py:15
  176.4 3.7 collective-permute-start.21
  178.8 5.0 collective-permute-start.20
  186.3 14.3 %copy-start.3 = (f32[18,1,64]{2,1,0:T(1,128)}, f32[18,1,64]{2,1,0:T(1,128)S(1)}, u32[]{:S(2)}) copy-start(f32[18,1,64]{2,1,0:T(1,128)S(1)} %reshape.1817) | copy-start | bytes 13828
  186.4 14.2 %copy-start.4 = (f32[18,1,64]{2,1,0:T(1,128)}, f32[18,1,64]{2,1,0:T(1,128)S(1)}, u32[]{:S(2)}) copy-start(f32[18,1,64]{2,1,0:T(1,128)S(1)} %reshape.1818) | copy-start | bytes 13828
  187.7 7.4 %collective-permute-start.22 = (f32[1641]{0:T(1024)S(1)}, f32[1641]{0:T(1024)S(1)}, u32[]{:S(2)}, u32[]{:S(2)}) collective-permute-start(f32[1641]{0:T(1024)S(1)} %concatenate.1135), channel_id=1, source_target_pairs={{1,0},{3,2},{5,4},{7,6},{9,8},{11,10},{13,12},{15,14},{17,16},{19,... | collective-permute-start | bytes 19700 | tf_op jit(solution)/shard_map/ppermute | solution.py:15
  190.2 5.9 %collective-permute-start.23 = (f32[1641]{0:T(1024)S(1)}, f32[1641]{0:T(1024)S(1)}, u32[]{:S(2)}, u32[]{:S(2)}) collective-permute-start(f32[1641]{0:T(1024)S(1)} %concatenate.1137), channel_id=1, source_target_pairs={{0,1},{2,3},{4,5},{6,7},{8,9},{10,11},{12,13},{14,15},{16,17},{18,... | collective-permute-start | bytes 19700 | tf_op jit(solution)/shard_map/ppermute | solution.py:15
  248.7 5.9 %collective-permute-start.24 = (f32[1,32,128]{2,0,1:T(1,128)S(1)}, f32[1,32,128]{2,0,1:T(1,128)S(1)}, u32[]{:S(2)}, u32[]{:S(2)}) collective-permute-start(f32[1,32,128]{2,0,1:T(1,128)S(1)} %get-tuple-element.153), channel_id=1, source_target_pairs={{8,0},{16,8},{24,16},{9,1},{17,9},{25,17},{10,2},{18,10},{26,18},{... | collective-permute-start | bytes 49160 | tf_op jit(solution)/shard_map/ppermute | solution.py:26
  250.0 6.0 %collective-permute-start.25 = (f32[1,32,128]{2,0,1:T(1,128)S(1)}, f32[1,32,128]{2,0,1:T(1,128)S(1)}, u32[]{:S(2)}, u32[]{:S(2)}) collective-permute-start(f32[1,32,128]{2,0,1:T(1,128)S(1)} %get-tuple-element.152), channel_id=1, source_target_pairs={{0,8},{8,16},{16,24},{1,9},{9,17},{17,25},{2,10},{10,18},{18,26},{... | collective-permute-start | bytes 49160 | tf_op jit(solution)/shard_map/ppermute | solution.py:25
  256.0 4.3 collective-permute-start.26
  257.3 3.9 collective-permute-start.27
  261.8 6.2 %collective-permute-start.28 = (f32[34,34,1]{1,2,0:T(1,128)S(1)}, f32[34,34,1]{1,2,0:T(1,128)S(1)}, u32[]{:S(2)}, u32[]{:S(2)}) collective-permute-start(f32[34,34,1]{1,2,0:T(1,128)S(1)} %copy.506), channel_id=1, source_target_pairs={{1,0},{3,2},{5,4},{7,6},{9,8},{11,10},{13,12},{15,14},{17,16},{19,... | collective-permute-start | bytes 13880 | tf_op jit(solution)/shard_map/ppermute | solution.py:26
  263.5 6.0 %collective-permute-start.29 = (f32[34,34,1]{1,2,0:T(1,128)S(1)}, f32[34,34,1]{1,2,0:T(1,128)S(1)}, u32[]{:S(2)}, u32[]{:S(2)}) collective-permute-start(f32[34,34,1]{1,2,0:T(1,128)S(1)} %copy.508), channel_id=1, source_target_pairs={{0,1},{2,3},{4,5},{6,7},{8,9},{10,11},{12,13},{14,15},{16,17},{18,... | collective-permute-start | bytes 13880 | tf_op jit(solution)/shard_map/ppermute | solution.py:25
  358.0 3.3 collective-permute-start.31
  360.0 5.7 collective-permute-start.30
  367.3 3.0 collective-permute-start.33
  369.0 5.4 collective-permute-start.32
  379.9 7.0 %collective-permute-start.34 = (f32[1641]{0:T(1024)S(1)}, f32[1641]{0:T(1024)S(1)}, u32[]{:S(2)}, u32[]{:S(2)}) collective-permute-start(f32[1641]{0:T(1024)S(1)} %concatenate.1193), channel_id=1, source_target_pairs={{1,0},{3,2},{5,4},{7,6},{9,8},{11,10},{13,12},{15,14},{17,16},{19,... | collective-permute-start | bytes 19700 | tf_op jit(solution)/shard_map/ppermute | solution.py:15
  382.3 5.9 %collective-permute-start.35 = (f32[1641]{0:T(1024)S(1)}, f32[1641]{0:T(1024)S(1)}, u32[]{:S(2)}, u32[]{:S(2)}) collective-permute-start(f32[1641]{0:T(1024)S(1)} %concatenate.1195), channel_id=1, source_target_pairs={{0,1},{2,3},{4,5},{6,7},{8,9},{10,11},{12,13},{14,15},{16,17},{18,... | collective-permute-start | bytes 19700 | tf_op jit(solution)/shard_map/ppermute | solution.py:15
  394.9 4.1 collective-permute-start.37
  397.7 5.8 %collective-permute-start.36 = (f32[5460]{0:T(1024)S(1)}, f32[5460]{0:T(1024)S(1)}, u32[]{:S(2)}, u32[]{:S(2)}) collective-permute-start(f32[5460]{0:T(1024)S(1)} %concatenate.1227), channel_id=1, source_target_pairs={{8,0},{16,8},{24,16},{9,1},{17,9},{25,17},{10,2},{18,10},{26,18},{... | collective-permute-start | bytes 65528 | tf_op jit(solution)/shard_map/ppermute | solution.py:15
  405.0 3.7 collective-permute-start.39
  407.4 5.0 collective-permute-start.38
  417.9 7.2 %collective-permute-start.40 = (f32[1641]{0:T(1024)S(1)}, f32[1641]{0:T(1024)S(1)}, u32[]{:S(2)}, u32[]{:S(2)}) collective-permute-start(f32[1641]{0:T(1024)S(1)} %concatenate.1243), channel_id=1, source_target_pairs={{1,0},{3,2},{5,4},{7,6},{9,8},{11,10},{13,12},{15,14},{17,16},{19,... | collective-permute-start | bytes 19700 | tf_op jit(solution)/shard_map/ppermute | solution.py:15
  420.5 5.9 %collective-permute-start.41 = (f32[1641]{0:T(1024)S(1)}, f32[1641]{0:T(1024)S(1)}, u32[]{:S(2)}, u32[]{:S(2)}) collective-permute-start(f32[1641]{0:T(1024)S(1)} %concatenate.1245), channel_id=1, source_target_pairs={{0,1},{2,3},{4,5},{6,7},{8,9},{10,11},{12,13},{14,15},{16,17},{18,... | collective-permute-start | bytes 19700 | tf_op jit(solution)/shard_map/ppermute | solution.py:15
  433.1 4.3 collective-permute-start.43
  436.1 5.8 %collective-permute-start.42 = (f32[5460]{0:T(1024)S(1)}, f32[5460]{0:T(1024)S(1)}, u32[]{:S(2)}, u32[]{:S(2)}) collective-permute-start(f32[5460]{0:T(1024)S(1)} %concatenate.1277), channel_id=1, source_target_pairs={{8,0},{16,8},{24,16},{9,1},{17,9},{25,17},{10,2},{18,10},{26,18},{... | collective-permute-start | bytes 65528 | tf_op jit(solution)/shard_map/ppermute | solution.py:15
  443.4 3.7 collective-permute-start.45
  445.9 5.0 collective-permute-start.44
  453.5 57.6 %copy-start.1 = (f32[34,1,128]{2,0,1:T(8,128)}, f32[34,1,128]{2,0,1:T(8,128)S(1)}, u32[]{:S(2)}) copy-start(f32[34,1,128]{2,0,1:T(8,128)S(1)} %slice_bitcast_fusion) | copy-start | bytes 52228
  456.3 7.0 %collective-permute-start.46 = (f32[1641]{0:T(1024)S(1)}, f32[1641]{0:T(1024)S(1)}, u32[]{:S(2)}, u32[]{:S(2)}) collective-permute-start(f32[1641]{0:T(1024)S(1)} %concatenate.1293), channel_id=1, source_target_pairs={{1,0},{3,2},{5,4},{7,6},{9,8},{11,10},{13,12},{15,14},{17,16},{19,... | collective-permute-start | bytes 19700 | tf_op jit(solution)/shard_map/ppermute | solution.py:15
  458.7 5.9 %collective-permute-start.47 = (f32[1641]{0:T(1024)S(1)}, f32[1641]{0:T(1024)S(1)}, u32[]{:S(2)}, u32[]{:S(2)}) collective-permute-start(f32[1641]{0:T(1024)S(1)} %concatenate.1295), channel_id=1, source_target_pairs={{0,1},{2,3},{4,5},{6,7},{8,9},{10,11},{12,13},{14,15},{16,17},{18,... | collective-permute-start | bytes 19700 | tf_op jit(solution)/shard_map/ppermute | solution.py:15
  514.0 5.9 %collective-permute-start.48 = (f32[1,32,128]{2,0,1:T(1,128)S(1)}, f32[1,32,128]{2,0,1:T(1,128)S(1)}, u32[]{:S(2)}, u32[]{:S(2)}) collective-permute-start(f32[1,32,128]{2,0,1:T(1,128)S(1)} %get-tuple-element.145), channel_id=1, source_target_pairs={{8,0},{16,8},{24,16},{9,1},{17,9},{25,17},{10,2},{18,10},{26,18},{... | collective-permute-start | bytes 49160 | tf_op jit(solution)/shard_map/ppermute | solution.py:26
  515.3 6.0 %collective-permute-start.49 = (f32[1,32,128]{2,0,1:T(1,128)S(1)}, f32[1,32,128]{2,0,1:T(1,128)S(1)}, u32[]{:S(2)}, u32[]{:S(2)}) collective-permute-start(f32[1,32,128]{2,0,1:T(1,128)S(1)} %get-tuple-element.144), channel_id=1, source_target_pairs={{0,8},{8,16},{16,24},{1,9},{9,17},{17,25},{2,10},{10,18},{18,26},{... | collective-permute-start | bytes 49160 | tf_op jit(solution)/shard_map/ppermute | solution.py:25
  521.3 4.3 collective-permute-start.50
  522.6 3.9 collective-permute-start.51
  527.8 6.2 %collective-permute-start.52 = (f32[34,34,1]{1,2,0:T(1,128)S(1)}, f32[34,34,1]{1,2,0:T(1,128)S(1)}, u32[]{:S(2)}, u32[]{:S(2)}) collective-permute-start(f32[34,34,1]{1,2,0:T(1,128)S(1)} %copy.612), channel_id=1, source_target_pairs={{1,0},{3,2},{5,4},{7,6},{9,8},{11,10},{13,12},{15,14},{17,16},{19,... | collective-permute-start | bytes 13880 | tf_op jit(solution)/shard_map/ppermute | solution.py:26
  529.4 6.0 %collective-permute-start.53 = (f32[34,34,1]{1,2,0:T(1,128)S(1)}, f32[34,34,1]{1,2,0:T(1,128)S(1)}, u32[]{:S(2)}, u32[]{:S(2)}) collective-permute-start(f32[34,34,1]{1,2,0:T(1,128)S(1)} %copy.614), channel_id=1, source_target_pairs={{0,1},{2,3},{4,5},{6,7},{8,9},{10,11},{12,13},{14,15},{16,17},{18,... | collective-permute-start | bytes 13880 | tf_op jit(solution)/shard_map/ppermute | solution.py:25
  (15 other events, 103.3 us)
